TPU v7x, 8 devices: a whole 2x2x1 slice. The times are simulated.
8 devices in a mesh: dp: 1 (over z), cx: 2 (over y), cy: 4 (over x, core).
Axes of the slice: x: 2, y: 2, z: 1, core: 2. Of those that a mesh axis runs over, the one named last changes fastest.
Arguments:
- x: bfloat16 [1, 2048, 1536], P('dp', ('cx', 'cy'))
- w_qkv: bfloat16 [1536, 4608], replicated
- w_o: bfloat16 [12, 128, 1536], replicated
Outputs:
- output: bfloat16 [1, 2048, 1536], P('dp', ('cx', 'cy'))
All inputs are finite; a program needn't handle non-finite values.
Results may differ from a plain program's by a relative error of at most 0.00801888.
Values are sent between devices in bfloat16 or wider.
A program may use at most 1 GiB of HBM per device.

v0:
```python
import jax
import jax.numpy as jnp
from jax import lax
from jax.sharding import PartitionSpec as P


def solution(mesh):
    def attend_local(x_blk, w_qkv, w_o):
        num_heads, head_dim = w_o.shape[0], w_o.shape[1]
        tok_rows = x_blk.shape[1]
        inv_sqrt = head_dim ** -0.5
        qkv_rows = jnp.dot(x_blk[0], w_qkv, preferred_element_type=jnp.float32).astype(jnp.bfloat16)
        qkv_rows = lax.all_to_all(qkv_rows.reshape(tok_rows, 3, num_heads, head_dim), "cy", 2, 0, tiled=True)
        kv_all = lax.all_gather(qkv_rows[:, 1:], "cx", axis=0, tiled=True)
        logits = jnp.einsum("qhd,khd->hqk", qkv_rows[:, 0], kv_all[:, 0], preferred_element_type=jnp.float32) * inv_sqrt
        row_max = jnp.max(logits, axis=-1, keepdims=True)
        weights = jnp.exp(logits - row_max)
        row_sum = jnp.sum(weights, axis=-1, keepdims=True)
        attn_rows = jnp.einsum("hqk,khd->qhd", weights.astype(jnp.bfloat16), kv_all[:, 1], preferred_element_type=jnp.float32)
        attn_rows = (attn_rows / jnp.transpose(row_sum, (1, 0, 2))).astype(jnp.bfloat16)
        attn_rows = lax.all_to_all(attn_rows, "cy", 0, 1, tiled=True)
        result = jnp.einsum("thd,hdc->tc", attn_rows, w_o, preferred_element_type=jnp.float32)
        return result.astype(jnp.bfloat16)[None]

    return jax.shard_map(attend_local, mesh=mesh, in_specs=(P("dp", ("cx", "cy"), None), P(None, None), P(None, None, None)), out_specs=P("dp", ("cx", "cy"), None), check_vma=False)
```

profile of v0, /device:TPU:0, one launch (start us, length us, event | category | flops | bytes accessed | tf_op | source)
XLA Modules:
  0.0 163.8 jit_solution(9118702683546910108)
XLA Ops:
  6.5 0.0 copy-start
  6.5 0.0 all-gather.2.cloned.1.call-start
  6.5 1.1 copy-done
  7.7 10.1 %convolution_convert_fusion = bf16[256,4608]{1,0:T(8,128)(2,1)} fusion(bf16[1536,4608]{1,0:T(8,128)(2,1)} %param.4, bf16[1,256,1536]{2,1,0:T(8,128)(2,1)S(1)} %copy-done), kind=kOutput, calls=%fused_computation.5 | convolution fusion | flops 3625058304 | bytes 17301504 | tf_op jit(solution)/shard_map/dot_general | solution.py:12
  17.8 2.8 %copy.12 = bf16[256,4608]{0,1:T(8,128)(2,1)S(1)} copy(bf16[256,4608]{1,0:T(8,128)(2,1)} %convolution_convert_fusion) | data formatting | bytes 4718592 | tf_op jit(solution)/shard_map/convert_element_type | solution.py:12
  20.6 0.2 copy.13
  20.9 32.9 %all_to_all.36 = bf16[256,3,12,128]{0,3,1,2:T(8,128)(2,1)} all-to-all(bf16[256,3,12,128]{0,3,1,2:T(8,128)(2,1)S(1)} %copy.13), channel_id=1, replica_groups=mesh['dp'=1,'cx'=2,'cy'=4] {'cy'}, dimensions={2} | all-to-all | bytes 4718592 | tf_op jit(solution)/shard_map/all_to_all | solution.py:13
  53.8 3.0 %copy.15 = bf16[4,256,3,3,128]{4,1,0,3,2:T(8,128)(2,1)S(1)} copy(bf16[4,256,3,3,128]{1,4,2,3,0:T(8,128)(2,1)} %bitcast.50) | data formatting | bytes 4718592 | tf_op jit(solution)/shard_map/all_to_all | solution.py:13
  56.8 1.3 slice.16
  58.1 0.0 all-gather.2.cloned.1.call-update
  58.1 43.0 %all-gather.2.cloned.1.call-done = bf16[2048,2,3,128]{3,0,2,1:T(8,128)(2,1)} async-done(((bf16[1024,2,3,128]{3,0,2,1:T(8,128)(2,1)}), bf16[2048,2,3,128]{3,0,2,1:T(8,128)(2,1)}) %all-gather.2.cloned.1.call-update) | async-done | bytes 3145744 | tf_op jit(solution)/shard_map/all_gather | solution.py:14
  101.1 11.5 %multiply_reduce_fusion = (f32[3,1024]{1,0:T(4,128)S(1)}, f32[3,1024,2048]{2,1,0:T(8,128)}) fusion(bf16[2048,2,3,128]{3,0,2,1:T(8,128)(2,1)} %all-gather.2.cloned.1.call-done, bf16[1024,3,3,128]{3,0,2,1:T(8,128)(2,1)S(1)} %bitcast.48), kind=kOutput, calls=%fused_computation.1 | convolution fusion | flops 1623192576 | bytes 27537408 | tf_op jit(solution)/shard_map/qhd,khd->hqk/dot_general | solution.py:15
  112.6 0.0 copy-start.1
  112.6 11.0 %fusion = f32[3,1024]{1,0:T(4,128)S(1)} fusion(f32[3,1024,2048]{2,1,0:T(8,128)} %get-tuple-element.6, f32[3,1024]{1,0:T(4,128)S(1)} %get-tuple-element.5), kind=kLoop, calls=%fused_computation.2 | loop fusion | flops 18871296 | bytes 25190400 | tf_op jit(solution)/shard_map/reduce_sum | solution.py:18
  123.6 0.0 copy-done.1
  123.6 10.9 %fusion.7 = bf16[1024,3,128]{0,2,1:T(8,128)(2,1)S(1)} fusion(f32[3,1024,2048]{2,1,0:T(8,128)} %get-tuple-element.6, f32[3,1024]{1,0:T(4,128)S(1)} %get-tuple-element.5, bf16[2048,2,3,128]{3,0,2,1:T(8,128)(2,1)S(1)} %copy-done.1, f32[1024,3]{0,1:T(4,128)S(1)} %bitcast.53), kind=kOutput, calls=%fused_computation.13 | convolution fusion | flops 1630273536 | bytes 27557888 | tf_op jit(solution)/shard_map/hqk,khd->qhd/dot_general | solution.py:19
  134.4 0.7 copy.17
  135.2 17.0 %all_to_all.37 = bf16[1024,3,128]{2,1,0:T(4,128)(2,1)S(1)} all-to-all(bf16[1024,3,128]{2,1,0:T(4,128)(2,1)S(1)} %copy.17), channel_id=1, replica_groups=mesh['dp'=1,'cx'=2,'cy'=4] {'cy'}, dimensions={0} | all-to-all | bytes 1572864 | tf_op jit(solution)/shard_map/all_to_all | solution.py:21
  152.2 0.2 copy.18
  152.3 4.6 %fusion.5 = bf16[1,256,1536]{2,1,0:T(8,128)(2,1)} fusion(bf16[256,12,128]{2,0,1:T(8,128)(2,1)S(1)} %bitcast.52, bf16[12,128,1536]{2,1,0:T(8,128)(2,1)} %param.5), kind=kOutput, calls=%fused_computation.8 | convolution fusion | flops 1208352768 | bytes 6291456 | tf_op jit(solution)/shard_map/thd,hdc->tc/dot_general | solution.py:22
Async XLA Ops:
  6.5 1.1 copy-start
  6.5 94.5 %all-gather.2.cloned.1.call-start = ((), (), s32[]{:S(2)}) async-start(), calls=%async_computation.2 | async-start | bytes 4718592 | tf_op jit(solution)/shard_map/all_gather | solution.py:14
  112.6 11.0 %copy-start.1 = (bf16[2048,2,3,128]{3,0,2,1:T(8,128)(2,1)S(1)}, bf16[2048,2,3,128]{3,0,2,1:T(8,128)(2,1)}, u32[]{:S(2)}) copy-start(bf16[2048,2,3,128]{3,0,2,1:T(8,128)(2,1)} %all-gather.2.cloned.1.call-done) | copy-start | bytes 9437188
Sparse Core Ops, SparseCore 0:
  58.2 42.7 all-gather.1
where the time goes:
time: 164 us
  blocking collectives  49.9 us (30%)
  waiting for transfers between devices  43 us (26%)
  matrix products  37.1 us (23%)
  between operations  13.5 us (8%)
  other arithmetic  11 us (7%)
  local copies, waits for them, and re-layouts  9.41 us (6%)
    all_gather x1, waiting for transfers between devices, attend_local(): kv_all = lax.all_gather(qkv_rows[:, 1:], 'cx', axis=0, tiled=True)  43 us
    all_to_all x1, blocking collectives, attend_local(): lax.all_to_all(qkv_rows.reshape(tok_rows, 3, num_heads, head_dim), 'cy',...  32.9 us
    all_to_all x1, blocking collectives, attend_local(): attn_rows = lax.all_to_all(attn_rows, 'cy', 0, 1, tiled=True)  17 us
    dot_general x1, matrix products, attend_local(): jnp.einsum('qhd,khd->hqk', qkv_rows[:, 0], kv_all[:, 0], preferred_elemen...  11.5 us
    reduce_sum x1, other arithmetic, attend_local(): row_sum = jnp.sum(weights, axis=-1, keepdims=True)  11 us
    dot_general x1, matrix products, attend_local(): jnp.einsum('hqk,khd->qhd', weights.astype(jnp.bfloat16), kv_all[:, 1], pr...  10.9 us
    dot_general x1, matrix products, attend_local(): jnp.dot(x_blk[0], w_qkv, preferred_element_type=jnp.float32)  10.1 us
    dot_general x1, matrix products, attend_local(): jnp.einsum('thd,hdc->tc', attn_rows, w_o, preferred_element_type=jnp.floa...  4.63 us
  transfers between devices with their start and end apart: 1, of which 1 were waited for; matrix products, arithmetic and copies ran while one was open for 0% of the time, Pallas kernels for 0%

commit v1 on v0

v1 whole, which is shorter than its diff:
```python
import functools
import math

import jax
import jax.numpy as jnp
from jax import lax
from jax.experimental import pallas as pl
from jax.experimental.pallas import tpu as pltpu
from jax.sharding import PartitionSpec as P

MESH = pl.DeviceIdType.MESH
BF16, F32 = jnp.bfloat16, jnp.float32
HEAD = 128


def kernel(x_hbm, wqkv_hbm, wo_hbm, y_ref,
           xbuf, wq, wk, wv, wo, qt, kbuf, vbuf, acc, mrow, lrow, osend, oown, oother, yacc,
           w_sem, own_sem, pair_sem, send_sem, fwd_sem, relay_sem, osend_sem,
           precv_sem, recv_sem, orecv_sem):
    tok, width = x_hbm.shape
    half = width // 2
    nh = half // HEAD
    quarter = tok // 4
    scale = math.log2(math.e) / math.sqrt(HEAD)

    dp, cx, cy = lax.axis_index("dp"), lax.axis_index("cx"), lax.axis_index("cy")
    core = lax.rem(cy, 2)
    partner = (dp, cx, cy + 1 - 2 * core)
    xnbr = (dp, cx, lax.rem(cy + 2, 4))
    ynbr = (dp, 1 - cx, cy)

    def wcopy(i, dst):
        cols = pl.ds(pl.multiple_of(i * width + core * half, HEAD), half)
        return pltpu.make_async_copy(wqkv_hbm.at[:, cols], dst, w_sem.at[i])

    xload = pltpu.make_async_copy(x_hbm, xbuf.at[0], own_sem)
    xload.start()
    wq_copy, wk_copy, wv_copy = wcopy(0, wq), wcopy(1, wk), wcopy(2, wv)
    wo_copy = pltpu.make_async_copy(wo_hbm, wo, w_sem.at[3])
    wq_copy.start()
    wk_copy.start()
    wv_copy.start()

    barrier = pltpu.get_barrier_semaphore()
    for nbr in (partner, xnbr, ynbr):
        pl.semaphore_signal(barrier, inc=1, device_id=nbr, device_id_type=MESH)
    pl.semaphore_wait(barrier, 3)

    def remote(src, dst, ssem, rsem, dev):
        return pltpu.make_async_remote_copy(src_ref=src, dst_ref=dst, send_sem=ssem, recv_sem=rsem,
                                            device_id=dev, device_id_type=MESH)

    def part(step, q):
        return xbuf.at[step, pl.ds(q * quarter, quarter), :]

    def own_rows(i):
        return xbuf.at[0, pl.ds(i * quarter, quarter), :]

    def xsend(i):
        return remote(own_rows((i + 2) % 4), part(2 + i, 0), send_sem.at[0, i], recv_sem.at[2 + i, 0], xnbr)

    def ysend(i):
        return remote(own_rows(i), part(2 + i, 2), send_sem.at[1, i], recv_sem.at[2 + i, 2], ynbr)

    pair_copy = remote(xbuf.at[0], xbuf.at[1], pair_sem, precv_sem, partner)

    def fwd(step, q):
        return remote(part(step, q), part(step, q + 1), fwd_sem.at[step, q // 2], recv_sem.at[step, q + 1], partner)

    def xrelay(step):
        return remote(part(step, 2), part(step + 4, 0), relay_sem.at[0, step], recv_sem.at[step + 4, 0], xnbr)

    def yrelay(step):
        return remote(part(step, 0), part(step + 4, 2), relay_sem.at[1, step], recv_sem.at[step + 4, 2], ynbr)

    def await_recv(step, q):
        remote(part(step, q), part(step, q), fwd_sem.at[step, 0], recv_sem.at[step, q], partner).wait_recv()

    xload.wait()
    for i in range(4):
        xsend(i).start()
        ysend(i).start()
        if i == 0:
            pair_copy.start()
    wo_copy.start()

    def dot(a, b):
        return jnp.dot(a, b, preferred_element_type=F32)

    def dot_t(a, b):
        return lax.dot_general(a, b, (((0,), (0,)), ((), ())), preferred_element_type=F32)

    def project_q(step):
        q = dot(xbuf[step], wq[...])
        for h in range(nh):
            qt[h, :, step * tok:(step + 1) * tok] = q[:, h * HEAD:(h + 1) * HEAD].T.astype(BF16)

    def project_kv(step):
        xs = xbuf[step]
        kbuf[...] = dot(xs, wk[...]).astype(BF16)
        vbuf[...] = dot(xs, wv[...]).astype(BF16)

    def attend():
        def logits(h):
            return dot(kbuf[:, h * HEAD:(h + 1) * HEAD], qt[h])

        s = logits(0)
        for h in range(nh):
            s_next = logits(h + 1) if h + 1 < nh else None
            m_old = mrow[h]
            m_new = jnp.maximum(m_old, jnp.max(s, axis=0, keepdims=True))
            p = jnp.exp2((s - m_new) * scale)
            a = jnp.exp2((m_old - m_new) * scale)
            lrow[h] = lrow[h] * a + jnp.sum(p, axis=0, keepdims=True)
            mrow[h] = m_new
            acc[h] = acc[h] * a + dot_t(vbuf[:, h * HEAD:(h + 1) * HEAD], p.astype(BF16))
            s = s_next

    acc[...] = jnp.zeros_like(acc)
    lrow[...] = jnp.zeros_like(lrow)
    mrow[...] = jnp.full(mrow.shape, -jnp.inf, F32)

    wq_copy.wait()
    project_q(0)
    wk_copy.wait()
    wv_copy.wait()
    project_kv(0)
    pair_copy.wait_recv()
    project_q(1)
    attend()
    project_kv(1)

    def body(step, carry):
        await_recv(step, 0)
        await_recv(step, 2)
        fwd(step, 0).start()
        fwd(step, 2).start()

        @pl.when(step < 4)
        def _():
            xrelay(step).start()
            yrelay(step).start()

        attend()
        await_recv(step, 1)
        await_recv(step, 3)
        project_kv(step)
        return carry

    lax.fori_loop(2, 8, body, 0)
    attend()

    def osend_copy(h):
        return remote(osend.at[h], oother.at[h], osend_sem.at[h], orecv_sem.at[h], partner)

    for h in range(nh):
        o = (acc[h] / lrow[h]).astype(BF16)
        oown[h * HEAD:(h + 1) * HEAD, :] = o[:, :tok]
        osend[h] = o[:, tok:]
    for h in range(nh):
        osend_copy(h).start()
    wo_copy.wait()
    own_rows_w = pl.ds(pl.multiple_of(core * half, HEAD), half)
    other_rows_w = pl.ds(pl.multiple_of((1 - core) * half, HEAD), half)
    yacc[...] = dot_t(oown[...], wo[own_rows_w, :])
    for h in range(nh):
        osend_copy(h).wait_recv()
    y_ref[...] = (yacc[...] + dot_t(oother[...].reshape(half, tok), wo[other_rows_w, :])).astype(BF16)

    pair_copy.wait_send()
    for i in range(4):
        xsend(i).wait_send()
        ysend(i).wait_send()
    for step in range(2, 8):
        fwd(step, 0).wait_send()
        fwd(step, 2).wait_send()
    for step in range(2, 4):
        xrelay(step).wait_send()
        yrelay(step).wait_send()
    for h in range(nh):
        osend_copy(h).wait_send()


def solution(mesh):
    def block(x, w_qkv, w_o):
        tok, width = x.shape[1], x.shape[2]
        half = width // 2
        nh = half // HEAD
        any_spec = pl.BlockSpec(memory_space=pl.ANY)
        dma = pltpu.SemaphoreType.DMA
        y = pl.pallas_call(
            kernel,
            out_shape=jax.ShapeDtypeStruct((tok, width), BF16),
            in_specs=[any_spec] * 3,
            out_specs=pl.BlockSpec(memory_space=pltpu.VMEM),
            scratch_shapes=[
                pltpu.VMEM((8, tok, width), BF16),
                pltpu.VMEM((width, half), BF16),
                pltpu.VMEM((width, half), BF16),
                pltpu.VMEM((width, half), BF16),
                pltpu.VMEM((width, width), BF16),
                pltpu.VMEM((nh, HEAD, 2 * tok), BF16),
                pltpu.VMEM((tok, half), BF16),
                pltpu.VMEM((tok, half), BF16),
                pltpu.VMEM((nh, HEAD, 2 * tok), F32),
                pltpu.VMEM((nh, 1, 2 * tok), F32),
                pltpu.VMEM((nh, 1, 2 * tok), F32),
                pltpu.VMEM((nh, HEAD, tok), BF16),
                pltpu.VMEM((half, tok), BF16),
                pltpu.VMEM((nh, HEAD, tok), BF16),
                pltpu.VMEM((tok, width), F32),
                dma((4,)), dma(()), dma(()), dma((2, 4)), dma((8, 2)), dma((2, 4)), dma((nh,)),
                dma(()), dma((8, 4)), dma((nh,)),
            ],
            compiler_params=pltpu.CompilerParams(
                collective_id=0, has_side_effects=True, vmem_limit_bytes=60 * 1024 * 1024),
            name="gather_attend",
        )(x[0], w_qkv, w_o.reshape(width, width))
        return y[None]

    return jax.shard_map(
        block, mesh=mesh,
        in_specs=(P("dp", ("cx", "cy"), None), P(None, None), P(None, None, None)),
        out_specs=P("dp", ("cx", "cy"), None), check_vma=False)
```

time: 164 us -> 41.1 us (0.25)
  blocking collectives: 49.9 us -> 0 us
  waiting for transfers between devices: 43 us -> 0 us
  Pallas kernels: 0 us -> 38.9 us
  matrix products: 37.1 us -> 0 us
  between operations: 13.5 us -> 0.01 us
  other arithmetic: 11 us -> 0 us
  local copies, waits for them, and re-layouts: 9.41 us -> 2.06 us
    all_to_all x2 -> x0, blocking collectives: 49.9 us -> none  [the longest x1 32.9 us: attend_local(): lax.all_to_all(qkv_rows.reshape(tok_rows, 3, num_heads, head_dim), 'cy',...]
    all_gather x1 -> x0, waiting for transfers between devices: 43 us -> none  [attend_local(): kv_all = lax.all_gather(qkv_rows[:, 1:], 'cx', axis=0, tiled=True)]
    pallas_call x0 -> x1, Pallas kernels: none -> 38.9 us  [block(): pl.pallas_call(kernel, out_shape=jax.ShapeDtypeStruct((tok, width), BF16)...]
    dot_general x4 -> x0, matrix products: 37.1 us -> none  [the longest x1 11.5 us: attend_local(): jnp.einsum('qhd,khd->hqk', qkv_rows[:, 0], kv_all[:, 0], preferred_elemen...]
    reduce_sum x1 -> x0, other arithmetic: 11 us -> none  [attend_local(): row_sum = jnp.sum(weights, axis=-1, keepdims=True)]
    convert_element_type x2 -> x0, local copies, waits for them, and re-layouts: 3.56 us -> none  [the longest x1 2.83 us: attend_local(): jnp.dot(x_blk[0], w_qkv, preferred_element_type=jnp.float32)]
    all_to_all x2 -> x0, local copies, waits for them, and re-layouts: 3.2 us -> none  [the longest x1 3.05 us: attend_local(): lax.all_to_all(qkv_rows.reshape(tok_rows, 3, num_heads, head_dim), 'cy',...]
  transfers between devices with their start and end apart: 1 -> 0, of which waited for: 1 -> 0; matrix products, arithmetic and copies ran while one was open for 0% -> 0% of each run, Pallas kernels for 0% -> 0%
where the time goes in v1:
time: 41.1 us; the launch traced here: 41 us
  Pallas kernels  38.9 us (95%)
  local copies, waits for them, and re-layouts  2.06 us (5%)
    pallas_call x1, Pallas kernels, block(): pl.pallas_call(kernel, out_shape=jax.ShapeDtypeStruct((tok, width), BF16)...  38.9 us
    unnamed x1, local copies, waits for them, and re-layouts  2.06 us

profile of v1, /device:TPU:0, one launch (start us, length us, event | category | flops | bytes accessed | tf_op | source)
XLA Modules:
  0.0 41.0 jit_solution(15822160789959579272)
XLA Ops:
  0.0 38.9 %gather_attend.1 = bf16[256,1536]{1,0:T(8,128)(2,1)} custom-call(bf16[256,1536]{1,0:T(8,128)(2,1)} %bitcast.5, bf16[1536,4608]{1,0:T(8,128)(2,1)} %wqkv_hbm.1, bf16[1536,1536]{1,0:T(8,128)(2,1)} %bitcast.3), custom_call_target="tpu_custom_call" | custom-call | tf_op jit(solution)/shard_map/gather_attend/pallas_call | solution.py:191
  38.9 2.1 %copy.5 = bf16[1,256,1536]{2,1,0:T(8,128)(2,1)} copy(bf16[1,256,1536]{2,1,0:T(8,128)(2,1)} %bitcast.4) | data formatting | bytes 1572864

commit v2 on v1

--- a/solution.py
+++ b/solution.py
@@ -34,24 +34,27 @@
         return pltpu.make_async_copy(wqkv_hbm.at[:, cols], dst, w_sem.at[i])
 
     xload = pltpu.make_async_copy(x_hbm, xbuf.at[0], own_sem)
-    xload.start()
     wq_copy, wk_copy, wv_copy = wcopy(0, wq), wcopy(1, wk), wcopy(2, wv)
     wo_copy = pltpu.make_async_copy(wo_hbm, wo, w_sem.at[3])
+    xload.start()
+
+    barrier = pltpu.get_barrier_semaphore()
+    for nbr in (partner, xnbr, ynbr):
+        pl.semaphore_signal(barrier, inc=1, device_id=nbr, device_id_type=MESH)
+    xload.wait()
     wq_copy.start()
     wk_copy.start()
     wv_copy.start()
-
-    barrier = pltpu.get_barrier_semaphore()
-    for nbr in (partner, xnbr, ynbr):
-        pl.semaphore_signal(barrier, inc=1, device_id=nbr, device_id_type=MESH)
     pl.semaphore_wait(barrier, 3)
 
     def remote(src, dst, ssem, rsem, dev):
         return pltpu.make_async_remote_copy(src_ref=src, dst_ref=dst, send_sem=ssem, recv_sem=rsem,
                                             device_id=dev, device_id_type=MESH)
 
-    def part(step, q):
-        return xbuf.at[step, pl.ds(q * quarter, quarter), :]
+    def part(step, q, sub=None):
+        if sub is None:
+            return xbuf.at[step, pl.ds(q * quarter, quarter), :]
+        return xbuf.at[step, pl.ds(sub * 2 * quarter + q * (quarter // 2), quarter // 2), :]
 
     def own_rows(i):
         return xbuf.at[0, pl.ds(i * quarter, quarter), :]
@@ -64,25 +67,28 @@
 
     pair_copy = remote(xbuf.at[0], xbuf.at[1], pair_sem, precv_sem, partner)
 
-    def fwd(step, q):
-        return remote(part(step, q), part(step, q + 1), fwd_sem.at[step, q // 2], recv_sem.at[step, q + 1], partner)
-
-    def xrelay(step):
-        return remote(part(step, 2), part(step + 4, 0), relay_sem.at[0, step], recv_sem.at[step + 4, 0], xnbr)
-
-    def yrelay(step):
-        return remote(part(step, 0), part(step + 4, 2), relay_sem.at[1, step], recv_sem.at[step + 4, 2], ynbr)
-
-    def await_recv(step, q):
-        remote(part(step, q), part(step, q), fwd_sem.at[step, 0], recv_sem.at[step, q], partner).wait_recv()
-
-    xload.wait()
+    def sem_of(step, sub):
+        return step if not sub else step + sub
+
+    def fwd(step, q, sub=None):
+        n = sem_of(step, sub)
+        return remote(part(step, q, sub), part(step, q + 1, sub), fwd_sem.at[n, q // 2], recv_sem.at[n, q + 1], partner)
+
+    def relay(q, step, sub=None):
+        n = sem_of(step + 4, sub)
+        rows = pl.ds(q * quarter + (sub or 0) * (quarter // 2), quarter if sub is None else quarter // 2)
+        return remote(xbuf.at[step, rows, :], part(step + 4, 2 - q, sub), relay_sem.at[q // 2, n], recv_sem.at[n, 2 - q],
+                      ynbr if q == 0 else xnbr)
+
+    def await_recv(step, q, sub=None):
+        n = sem_of(step, sub)
+        remote(part(step, q, sub), part(step, q, sub), fwd_sem.at[n, 0], recv_sem.at[n, q], partner).wait_recv()
+
     for i in range(4):
         xsend(i).start()
         ysend(i).start()
         if i == 0:
             pair_copy.start()
-    wo_copy.start()
 
     def dot(a, b):
         return jnp.dot(a, b, preferred_element_type=F32)
@@ -95,25 +101,32 @@
         for h in range(nh):
             qt[h, :, step * tok:(step + 1) * tok] = q[:, h * HEAD:(h + 1) * HEAD].T.astype(BF16)
 
-    def project_kv(step):
-        xs = xbuf[step]
-        kbuf[...] = dot(xs, wk[...]).astype(BF16)
-        vbuf[...] = dot(xs, wv[...]).astype(BF16)
-
-    def attend():
+    def project_kv(step, sub=None):
+        rows = slice(0, tok) if sub is None else slice(sub * tok // 2, (sub + 1) * tok // 2)
+        keys = slice(0, rows.stop - rows.start)
+        xs = xbuf[step, rows, :]
+        kbuf[keys, :] = dot(xs, wk[...]).astype(BF16)
+        vbuf[keys, :] = dot(xs, wv[...]).astype(BF16)
+
+    def attend(keys=tok, qs=slice(0, 2 * tok), after=None):
         def logits(h):
-            return dot(kbuf[:, h * HEAD:(h + 1) * HEAD], qt[h])
+            return dot(kbuf[0:keys, h * HEAD:(h + 1) * HEAD], qt[h, :, qs])
 
         s = logits(0)
         for h in range(nh):
             s_next = logits(h + 1) if h + 1 < nh else None
-            m_old = mrow[h]
+            m_old = mrow[h, :, qs]
             m_new = jnp.maximum(m_old, jnp.max(s, axis=0, keepdims=True))
             p = jnp.exp2((s - m_new) * scale)
             a = jnp.exp2((m_old - m_new) * scale)
-            lrow[h] = lrow[h] * a + jnp.sum(p, axis=0, keepdims=True)
-            mrow[h] = m_new
-            acc[h] = acc[h] * a + dot_t(vbuf[:, h * HEAD:(h + 1) * HEAD], p.astype(BF16))
+            l_new = lrow[h, :, qs] * a + jnp.sum(p, axis=0, keepdims=True)
+            o_new = acc[h, :, qs] * a + dot_t(vbuf[0:keys, h * HEAD:(h + 1) * HEAD], p.astype(BF16))
+            if after is None:
+                lrow[h, :, qs] = l_new
+                mrow[h, :, qs] = m_new
+                acc[h, :, qs] = o_new
+            else:
+                after(h, (o_new / l_new).astype(BF16))
             s = s_next
 
     acc[...] = jnp.zeros_like(acc)
@@ -124,6 +137,7 @@
     project_q(0)
     wk_copy.wait()
     wv_copy.wait()
+    wo_copy.start()
     project_kv(0)
     pair_copy.wait_recv()
     project_q(1)
@@ -136,10 +150,16 @@
         fwd(step, 0).start()
         fwd(step, 2).start()
 
-        @pl.when(step < 4)
+        @pl.when(step == 2)
         def _():
-            xrelay(step).start()
-            yrelay(step).start()
+            relay(2, 2).start()
+            relay(0, 2).start()
+
+        @pl.when(step == 3)
+        def _():
+            for sub in range(2):
+                relay(2, 3, sub).start()
+                relay(0, 3, sub).start()
 
         attend()
         await_recv(step, 1)
@@ -147,19 +167,36 @@
         project_kv(step)
         return carry
 
-    lax.fori_loop(2, 8, body, 0)
-    attend()
+    lax.fori_loop(2, 7, body, 0)
+    for sub in range(2):
+        await_recv(7, 0, sub)
+        await_recv(7, 2, sub)
+        fwd(7, 0, sub).start()
+        fwd(7, 2, sub).start()
+        if sub == 0:
+            attend()
+        else:
+            attend(keys=tok // 2)
+        await_recv(7, 1, sub)
+        await_recv(7, 3, sub)
+        project_kv(7, sub)
 
     def osend_copy(h):
         return remote(osend.at[h], oother.at[h], osend_sem.at[h], orecv_sem.at[h], partner)
 
-    for h in range(nh):
-        o = (acc[h] / lrow[h]).astype(BF16)
-        oown[h * HEAD:(h + 1) * HEAD, :] = o[:, :tok]
-        osend[h] = o[:, tok:]
-    for h in range(nh):
-        osend_copy(h).start()
+    def give(h, o):
+        osend[h] = o
+        if h > 0:
+            osend_copy(h - 1).start()
+
+    def keep(h, o):
+        oown[h * HEAD:(h + 1) * HEAD, :] = o
+        if h == 0:
+            osend_copy(nh - 1).start()
+
+    attend(keys=tok // 2, qs=slice(tok, 2 * tok), after=give)
     wo_copy.wait()
+    attend(keys=tok // 2, qs=slice(0, tok), after=keep)
     own_rows_w = pl.ds(pl.multiple_of(core * half, HEAD), half)
     other_rows_w = pl.ds(pl.multiple_of((1 - core) * half, HEAD), half)
     yacc[...] = dot_t(oown[...], wo[own_rows_w, :])
@@ -171,12 +208,12 @@
     for i in range(4):
         xsend(i).wait_send()
         ysend(i).wait_send()
-    for step in range(2, 8):
-        fwd(step, 0).wait_send()
-        fwd(step, 2).wait_send()
-    for step in range(2, 4):
-        xrelay(step).wait_send()
-        yrelay(step).wait_send()
+    for step, sub in [(s, None) for s in range(2, 7)] + [(7, 0), (7, 1)]:
+        fwd(step, 0, sub).wait_send()
+        fwd(step, 2, sub).wait_send()
+    for step, sub in [(2, None), (3, 0), (3, 1)]:
+        relay(0, step, sub).wait_send()
+        relay(2, step, sub).wait_send()
     for h in range(nh):
         osend_copy(h).wait_send()
 
@@ -209,11 +246,11 @@
                 pltpu.VMEM((half, tok), BF16),
                 pltpu.VMEM((nh, HEAD, tok), BF16),
                 pltpu.VMEM((tok, width), F32),
-                dma((4,)), dma(()), dma(()), dma((2, 4)), dma((8, 2)), dma((2, 4)), dma((nh,)),
-                dma(()), dma((8, 4)), dma((nh,)),
+                dma((4,)), dma(()), dma(()), dma((2, 4)), dma((9, 2)), dma((2, 9)), dma((nh,)),
+                dma(()), dma((9, 4)), dma((nh,)),
             ],
             compiler_params=pltpu.CompilerParams(
-                collective_id=0, has_side_effects=True, vmem_limit_bytes=60 * 1024 * 1024),
+                collective_id=0, has_side_effects=True, vmem_limit_bytes=53 * 1024 * 1024),
             name="gather_attend",
         )(x[0], w_qkv, w_o.reshape(width, width))
         return y[None]

time: 41.1 us -> 39.7 us (0.966)
  local copies, waits for them, and re-layouts: 2.06 us -> 0.88 us
    unnamed x1, local copies, waits for them, and re-layouts: 2.06 us -> 0.88 us
where the time goes in v2:
time: 39.7 us; the launch traced here: 39.6 us
  Pallas kernels  38.7 us (97%)
  local copies, waits for them, and re-layouts  0.88 us (2%)
    pallas_call x1, Pallas kernels, block(): pl.pallas_call(kernel, out_shape=jax.ShapeDtypeStruct((tok, width), BF16)...  38.7 us
    unnamed x1, local copies, waits for them, and re-layouts  0.88 us

profile of v2, /device:TPU:0, one launch (start us, length us, event | category | flops | bytes accessed | tf_op | source)
XLA Modules:
  0.0 39.6 jit_solution(4410694847635052840)
XLA Ops:
  0.0 38.7 %gather_attend.1 = bf16[256,1536]{1,0:T(8,128)(2,1)S(1)} custom-call(bf16[256,1536]{1,0:T(8,128)(2,1)} %bitcast.5, bf16[1536,4608]{1,0:T(8,128)(2,1)} %wqkv_hbm.1, bf16[1536,1536]{1,0:T(8,128)(2,1)} %bitcast.4), custom_call_target="tpu_custom_call" | custom-call | tf_op jit(solution)/shard_map/gather_attend/pallas_call | solution.py:228
  38.7 0.9 %copy.5 = bf16[1,256,1536]{2,1,0:T(8,128)(2,1)} copy(bf16[1,256,1536]{2,1,0:T(8,128)(2,1)S(1)} %bitcast.3) | data formatting | bytes 1572864

commit v3 on v2

--- a/solution.py
+++ b/solution.py
@@ -57,10 +57,13 @@
         return xbuf.at[step, pl.ds(sub * 2 * quarter + q * (quarter // 2), quarter // 2), :]
 
     def own_rows(i):
-        return xbuf.at[0, pl.ds(i * quarter, quarter), :]
+        start = i * quarter
+        if not isinstance(i, int):
+            start = pl.multiple_of(start, quarter)
+        return xbuf.at[0, pl.ds(start, quarter), :]
 
     def xsend(i):
-        return remote(own_rows((i + 2) % 4), part(2 + i, 0), send_sem.at[0, i], recv_sem.at[2 + i, 0], xnbr)
+        return remote(own_rows((i + 2) % 4 if isinstance(i, int) else lax.rem(i + 2, 4)), part(2 + i, 0), send_sem.at[0, i], recv_sem.at[2 + i, 0], xnbr)
 
     def ysend(i):
         return remote(own_rows(i), part(2 + i, 2), send_sem.at[1, i], recv_sem.at[2 + i, 2], ynbr)
@@ -84,7 +87,7 @@
         n = sem_of(step, sub)
         remote(part(step, q, sub), part(step, q, sub), fwd_sem.at[n, 0], recv_sem.at[n, q], partner).wait_recv()
 
-    for i in range(4):
+    for i in range(2):
         xsend(i).start()
         ysend(i).start()
         if i == 0:
@@ -150,16 +153,25 @@
         fwd(step, 0).start()
         fwd(step, 2).start()
 
-        @pl.when(step == 2)
+        @pl.when(step < 4)
+        def _():
+            xsend(step).start()
+            ysend(step).start()
+
+        @pl.when(step == 4)
         def _():
             relay(2, 2).start()
             relay(0, 2).start()
 
-        @pl.when(step == 3)
-        def _():
-            for sub in range(2):
-                relay(2, 3, sub).start()
-                relay(0, 3, sub).start()
+        @pl.when(step == 5)
+        def _():
+            relay(2, 3, 0).start()
+            relay(0, 3, 0).start()
+
+        @pl.when(step == 6)
+        def _():
+            relay(2, 3, 1).start()
+            relay(0, 3, 1).start()
 
         attend()
         await_recv(step, 1)

time: 39.7 us -> 39.3 us (0.990)
  Pallas kernels: 38.7 us -> 38.2 us
    pallas_call x1, Pallas kernels: 38.7 us -> 38.2 us  [block(): pl.pallas_call(kernel, out_shape=jax.ShapeDtypeStruct((tok, width), BF16)...]
where the time goes in v3:
time: 39.3 us; the launch traced here: 39.1 us
  Pallas kernels  38.2 us (97%)
  local copies, waits for them, and re-layouts  0.88 us (2%)
    pallas_call x1, Pallas kernels, block(): pl.pallas_call(kernel, out_shape=jax.ShapeDtypeStruct((tok, width), BF16)...  38.2 us
    unnamed x1, local copies, waits for them, and re-layouts  0.88 us

profile of v3, /device:TPU:0, one launch (start us, length us, event | category | flops | bytes accessed | tf_op | source)
XLA Modules:
  0.0 39.1 jit_solution(6455153272356914849)
XLA Ops:
  0.0 38.2 %gather_attend.1 = bf16[256,1536]{1,0:T(8,128)(2,1)S(1)} custom-call(bf16[256,1536]{1,0:T(8,128)(2,1)} %bitcast.5, bf16[1536,4608]{1,0:T(8,128)(2,1)} %wqkv_hbm.1, bf16[1536,1536]{1,0:T(8,128)(2,1)} %bitcast.4), custom_call_target="tpu_custom_call" | custom-call | tf_op jit(solution)/shard_map/gather_attend/pallas_call | solution.py:240
  38.2 0.9 %copy.5 = bf16[1,256,1536]{2,1,0:T(8,128)(2,1)} copy(bf16[1,256,1536]{2,1,0:T(8,128)(2,1)S(1)} %bitcast.3) | data formatting | bytes 1572864

commit v4 on v3

--- a/solution.py
+++ b/solution.py
@@ -14,7 +14,7 @@
 
 
 def kernel(x_hbm, wqkv_hbm, wo_hbm, y_ref,
-           xbuf, wq, wk, wv, wo, qt, kbuf, vbuf, acc, mrow, lrow, osend, oown, oother, yacc,
+           xbuf, wq, wk, wv, wo, qt, kbuf0, kbuf1, vbuf0, vbuf1, acc, mrow, lrow, osend, oown, oother, yacc,
            w_sem, own_sem, pair_sem, send_sem, fwd_sem, relay_sem, osend_sem,
            precv_sem, recv_sem, orecv_sem):
     tok, width = x_hbm.shape
@@ -87,11 +87,36 @@
         n = sem_of(step, sub)
         remote(part(step, q, sub), part(step, q, sub), fwd_sem.at[n, 0], recv_sem.at[n, q], partner).wait_recv()
 
-    for i in range(2):
-        xsend(i).start()
-        ysend(i).start()
+    out_x = [xsend(i) for i in range(4)] + [relay(2, 2), relay(2, 3, 0), relay(2, 3, 1)]
+    out_y = [ysend(i) for i in range(4)] + [relay(0, 2), relay(0, 3, 0), relay(0, 3, 1)]
+    depth = 3
+    for i in range(depth):
+        out_x[i].start()
+        out_y[i].start()
         if i == 0:
             pair_copy.start()
+
+    chunks = [(0, None), (1, None)] + [(s, None) for s in range(2, 7)] + [(7, 0), (7, 1)]
+    kbufs, vbufs = (kbuf0, kbuf1), (vbuf0, vbuf1)
+
+    def nkeys(c):
+        return tok if chunks[c][1] is None else tok // 2
+
+    def arrive(c):
+        step, sub = chunks[c]
+        await_recv(step, 0, sub)
+        await_recv(step, 2, sub)
+        fwd(step, 0, sub).start()
+        fwd(step, 2, sub).start()
+        i = c - 2 + depth
+        if i < len(out_x):
+            out_x[i].start()
+            out_y[i].start()
+
+    def twins(c):
+        step, sub = chunks[c]
+        await_recv(step, 1, sub)
+        await_recv(step, 3, sub)
 
     def dot(a, b):
         return jnp.dot(a, b, preferred_element_type=F32)
@@ -104,16 +129,24 @@
         for h in range(nh):
             qt[h, :, step * tok:(step + 1) * tok] = q[:, h * HEAD:(h + 1) * HEAD].T.astype(BF16)
 
-    def project_kv(step, sub=None):
-        rows = slice(0, tok) if sub is None else slice(sub * tok // 2, (sub + 1) * tok // 2)
-        keys = slice(0, rows.stop - rows.start)
-        xs = xbuf[step, rows, :]
-        kbuf[keys, :] = dot(xs, wk[...]).astype(BF16)
-        vbuf[keys, :] = dot(xs, wv[...]).astype(BF16)
-
-    def attend(keys=tok, qs=slice(0, 2 * tok), after=None):
+    piece = 2 * HEAD
+
+    def project_pieces(c):
+        step, sub = chunks[c]
+        n = nkeys(c)
+        row0 = 0 if not sub else sub * n
+        for w, buf in ((wk, kbufs[c % 2]), (wv, vbufs[c % 2])):
+            for j in range(half // piece):
+                cols = slice(j * piece, (j + 1) * piece)
+                buf[0:n, cols] = dot(xbuf[step, row0:row0 + n, :], w[:, cols]).astype(BF16)
+                yield
+
+    def attend_heads(c, qs=slice(0, 2 * tok), after=None):
+        n = nkeys(c)
+        kb, vb = kbufs[c % 2], vbufs[c % 2]
+
         def logits(h):
-            return dot(kbuf[0:keys, h * HEAD:(h + 1) * HEAD], qt[h, :, qs])
+            return dot(kb[0:n, h * HEAD:(h + 1) * HEAD], qt[h, :, qs])
 
         s = logits(0)
         for h in range(nh):
@@ -123,14 +156,22 @@
             p = jnp.exp2((s - m_new) * scale)
             a = jnp.exp2((m_old - m_new) * scale)
             l_new = lrow[h, :, qs] * a + jnp.sum(p, axis=0, keepdims=True)
-            o_new = acc[h, :, qs] * a + dot_t(vbuf[0:keys, h * HEAD:(h + 1) * HEAD], p.astype(BF16))
+            o_new = acc[h, :, qs] * a + dot_t(vb[0:n, h * HEAD:(h + 1) * HEAD], p.astype(BF16))
             if after is None:
                 lrow[h, :, qs] = l_new
                 mrow[h, :, qs] = m_new
                 acc[h, :, qs] = o_new
             else:
-                after(h, (o_new / l_new).astype(BF16))
+                after(h, (o_new * (1.0 / l_new)).astype(BF16))
             s = s_next
+            yield
+
+    def run(*gens):
+        gens = list(gens)
+        while gens:
+            for g in list(gens):
+                if next(g, gens) is gens:
+                    gens.remove(g)
 
     acc[...] = jnp.zeros_like(acc)
     lrow[...] = jnp.zeros_like(lrow)
@@ -141,57 +182,41 @@
     wk_copy.wait()
     wv_copy.wait()
     wo_copy.start()
-    project_kv(0)
+    run(project_pieces(0))
     pair_copy.wait_recv()
     project_q(1)
-    attend()
-    project_kv(1)
-
-    def body(step, carry):
-        await_recv(step, 0)
-        await_recv(step, 2)
-        fwd(step, 0).start()
-        fwd(step, 2).start()
-
-        @pl.when(step < 4)
-        def _():
-            xsend(step).start()
-            ysend(step).start()
-
-        @pl.when(step == 4)
-        def _():
-            relay(2, 2).start()
-            relay(0, 2).start()
-
-        @pl.when(step == 5)
-        def _():
-            relay(2, 3, 0).start()
-            relay(0, 3, 0).start()
-
-        @pl.when(step == 6)
-        def _():
-            relay(2, 3, 1).start()
-            relay(0, 3, 1).start()
-
-        attend()
-        await_recv(step, 1)
-        await_recv(step, 3)
-        project_kv(step)
-        return carry
-
-    lax.fori_loop(2, 7, body, 0)
-    for sub in range(2):
-        await_recv(7, 0, sub)
-        await_recv(7, 2, sub)
-        fwd(7, 0, sub).start()
-        fwd(7, 2, sub).start()
-        if sub == 0:
-            attend()
-        else:
-            attend(keys=tok // 2)
-        await_recv(7, 1, sub)
-        await_recv(7, 3, sub)
-        project_kv(7, sub)
+    run(project_pieces(1), attend_heads(0))
+    for c in range(2, 6):
+        arrive(c)
+        twins(c)
+        run(project_pieces(c), attend_heads(c - 1))
+    arrive(6)
+    run(attend_heads(5))
+    twins(6)
+    pair_copy.wait_send()
+    for i in range(4):
+        xsend(i).wait_send()
+        ysend(i).wait_send()
+    for c in range(2, 6):
+        fwd(*[chunks[c][0], 0]).wait_send()
+        fwd(*[chunks[c][0], 2]).wait_send()
+    arrive(7)
+    run(project_pieces(6))
+    twins(7)
+    for step in (2, 3):
+        sub = None if step == 2 else 0
+        relay(0, step, sub).wait_send()
+        relay(2, step, sub).wait_send()
+    fwd(6, 0).wait_send()
+    fwd(6, 2).wait_send()
+    arrive(8)
+    run(project_pieces(7), attend_heads(6))
+    twins(8)
+    for q in (0, 2):
+        relay(q, 3, 1).wait_send()
+        fwd(7, q, 0).wait_send()
+        fwd(7, q, 1).wait_send()
+    run(project_pieces(8), attend_heads(7))
 
     def osend_copy(h):
         return remote(osend.at[h], oother.at[h], osend_sem.at[h], orecv_sem.at[h], partner)
@@ -206,9 +231,9 @@
         if h == 0:
             osend_copy(nh - 1).start()
 
-    attend(keys=tok // 2, qs=slice(tok, 2 * tok), after=give)
     wo_copy.wait()
-    attend(keys=tok // 2, qs=slice(0, tok), after=keep)
+    run(attend_heads(8, slice(tok, 2 * tok), give))
+    run(attend_heads(8, slice(0, tok), keep))
     own_rows_w = pl.ds(pl.multiple_of(core * half, HEAD), half)
     other_rows_w = pl.ds(pl.multiple_of((1 - core) * half, HEAD), half)
     yacc[...] = dot_t(oown[...], wo[own_rows_w, :])
@@ -216,16 +241,6 @@
         osend_copy(h).wait_recv()
     y_ref[...] = (yacc[...] + dot_t(oother[...].reshape(half, tok), wo[other_rows_w, :])).astype(BF16)
 
-    pair_copy.wait_send()
-    for i in range(4):
-        xsend(i).wait_send()
-        ysend(i).wait_send()
-    for step, sub in [(s, None) for s in range(2, 7)] + [(7, 0), (7, 1)]:
-        fwd(step, 0, sub).wait_send()
-        fwd(step, 2, sub).wait_send()
-    for step, sub in [(2, None), (3, 0), (3, 1)]:
-        relay(0, step, sub).wait_send()
-        relay(2, step, sub).wait_send()
     for h in range(nh):
         osend_copy(h).wait_send()
 
@@ -251,6 +266,8 @@
                 pltpu.VMEM((nh, HEAD, 2 * tok), BF16),
                 pltpu.VMEM((tok, half), BF16),
                 pltpu.VMEM((tok, half), BF16),
+                pltpu.VMEM((tok, half), BF16),
+                pltpu.VMEM((tok, half), BF16),
                 pltpu.VMEM((nh, HEAD, 2 * tok), F32),
                 pltpu.VMEM((nh, 1, 2 * tok), F32),
                 pltpu.VMEM((nh, 1, 2 * tok), F32),

time: 39.3 us -> 39.3 us (level)
  no operation moved by 1% of the time
where the time goes in v4:
time: 39.3 us; the launch traced here: 39.2 us
  Pallas kernels  38.3 us (97%)
  local copies, waits for them, and re-layouts  0.88 us (2%)
    pallas_call x1, Pallas kernels, block(): pl.pallas_call(kernel, out_shape=jax.ShapeDtypeStruct((tok, width), BF16)...  38.3 us
    unnamed x1, local copies, waits for them, and re-layouts  0.88 us

profile of v4, /device:TPU:0, one launch (start us, length us, event | category | flops | bytes accessed | tf_op | source)
XLA Modules:
  0.0 39.2 jit_solution(16773372543275792822)
XLA Ops:
  0.0 38.3 %gather_attend.1 = bf16[256,1536]{1,0:T(8,128)(2,1)S(1)} custom-call(bf16[256,1536]{1,0:T(8,128)(2,1)} %bitcast.5, bf16[1536,4608]{1,0:T(8,128)(2,1)} %wqkv_hbm.1, bf16[1536,1536]{1,0:T(8,128)(2,1)} %bitcast.4), custom_call_target="tpu_custom_call" | custom-call | tf_op jit(solution)/shard_map/gather_attend/pallas_call | solution.py:255
  38.3 0.9 %copy.5 = bf16[1,256,1536]{2,1,0:T(8,128)(2,1)} copy(bf16[1,256,1536]{2,1,0:T(8,128)(2,1)S(1)} %bitcast.3) | data formatting | bytes 1572864

commit v5 on v0

v5 whole, which is shorter than its diff:
```python
import math

import jax
import jax.numpy as jnp
from jax import lax
from jax.experimental import pallas as pl
from jax.experimental.pallas import tpu as pltpu
from jax.sharding import PartitionSpec as P

MESH = pl.DeviceIdType.MESH
BF16, F32 = jnp.bfloat16, jnp.float32
HEAD = 128


def kernel(x_hbm, wqkv_hbm, wo_hbm, y_ref,
           xbuf, wq, wk, wv, wo, qt, kbuf0, kbuf1, vbuf0, vbuf1, acc, mrow, lrow, osend, oown, oother, facc,
           w_sem, x_sem, pair_sem, send_sem, osend_sem, link_sem, twin_sem, orecv_sem):
    tok, width = x_hbm.shape
    half = width // 2
    nh = half // HEAD
    quarter = tok // 4
    scale = math.log2(math.e) / math.sqrt(HEAD)

    dp, cx, cy = lax.axis_index("dp"), lax.axis_index("cx"), lax.axis_index("cy")
    core = lax.rem(cy, 2)
    partner = (dp, cx, cy + 1 - 2 * core)
    xnbr = (dp, cx, lax.rem(cy + 2, 4))
    ynbr = (dp, 1 - cx, cy)

    def wcopy(i, dst):
        cols = pl.ds(pl.multiple_of(i * width + core * half, HEAD), half)
        return pltpu.make_async_copy(wqkv_hbm.at[:, cols], dst, w_sem.at[i])

    wq_copy, wk_copy, wv_copy = wcopy(0, wq), wcopy(1, wk), wcopy(2, wv)
    wo_copy = pltpu.make_async_copy(wo_hbm, wo, w_sem.at[3])

    def own_rows(i, n=1):
        return xbuf.at[0, pl.ds(i * quarter, n * quarter), :]

    for i in (2, 0, 3, 1):
        pltpu.make_async_copy(x_hbm.at[pl.ds(i * quarter, quarter), :], own_rows(i), x_sem.at[i % 2]).start()

    def xload_wait(i):
        pltpu.make_async_copy(x_hbm.at[pl.ds(0, 2 * quarter), :], own_rows(0, 2), x_sem.at[i]).wait()

    barrier = pltpu.get_barrier_semaphore()
    for nbr in (partner, xnbr, ynbr):
        pl.semaphore_signal(barrier, inc=1, device_id=nbr, device_id_type=MESH)
    acc[...] = jnp.zeros_like(acc)
    lrow[...] = jnp.zeros_like(lrow)
    mrow[...] = jnp.full(mrow.shape, -jnp.inf, F32)
    wq_copy.start()
    xload_wait(0)
    pl.semaphore_wait(barrier, 3)

    pieces = [(c, slice(0, width)) for c in range(2, 7)] + [(7, slice(0, half)), (7, slice(half, width))]

    def part(c, q, cols):
        return xbuf.at[c, q * quarter:(q + 1) * quarter, cols]

    def remote(src, dst, ssem, rsem, dev):
        return pltpu.make_async_remote_copy(src_ref=src, dst_ref=dst, send_sem=ssem, recv_sem=rsem,
                                            device_id=dev, device_id_type=MESH)

    def link_copy(i, q):
        c, cols = pieces[i]
        dev = xnbr if q == 0 else ynbr
        if c < 6:
            src = own_rows((c if q == 0 else c - 2) % 4)
        else:
            src = part(c - 4, 2 - q, cols)
        return remote(src, part(c, q, cols), send_sem, link_sem.at[i], dev)

    def twin_copy(i, q):
        c, cols = pieces[i]
        return remote(part(c, q, cols), part(c, q + 1, cols), send_sem, twin_sem.at[i], partner)

    pair_copy = remote(xbuf.at[0], xbuf.at[1], send_sem, pair_sem, partner)
    depth = 3

    def send(i):
        if i < len(pieces):
            link_copy(i, 0).start()
            link_copy(i, 2).start()

    def both_parts(i, sems):
        c, cols = pieces[i]
        both = xbuf.at[c, 0:2 * quarter, cols]
        return remote(both, both, send_sem, sems.at[i], partner)

    def arrive(i):
        both_parts(i, link_sem).wait_recv()
        twin_copy(i, 0).start()
        twin_copy(i, 2).start()
        send(i + depth)

    def twins(i):
        both_parts(i, twin_sem).wait_recv()

    send(0)
    xload_wait(1)
    for i in range(1, depth):
        send(i)
    pair_copy.start()
    wk_copy.start()
    wv_copy.start()

    def dot(a, b):
        return jnp.dot(a, b, preferred_element_type=F32)

    def dot_t(a, b):
        return lax.dot_general(a, b, (((0,), (0,)), ((), ())), preferred_element_type=F32)

    kbufs, vbufs = (kbuf0, kbuf1), (vbuf0, vbuf1)

    def project_q(c):
        q = dot(xbuf[c], wq[...])
        for h in range(nh):
            qt[h, :, c * tok:(c + 1) * tok] = q[:, h * HEAD:(h + 1) * HEAD].T.astype(BF16)

    def project(c):
        xs = xbuf[c]
        kbufs[c % 2][...] = dot(xs, wk[...]).astype(BF16)
        vbufs[c % 2][...] = dot(xs, wv[...]).astype(BF16)

    def project_first(c):
        xs = xbuf[c, :, 0:half]
        facc[:, 0:half] = dot(xs, wk[0:half, :])
        facc[:, half:] = dot(xs, wv[0:half, :])

    def project_second(c):
        xs = xbuf[c, :, half:]
        kbufs[c % 2][...] = (facc[:, 0:half] + dot(xs, wk[half:, :])).astype(BF16)
        vbufs[c % 2][...] = (facc[:, half:] + dot(xs, wv[half:, :])).astype(BF16)

    def attend(c, heads=range(nh), qs=slice(0, 2 * tok), out=None):
        kb, vb = kbufs[c % 2], vbufs[c % 2]

        def logits(h):
            return dot(kb[:, h * HEAD:(h + 1) * HEAD], qt[h, :, qs])

        s = logits(heads[0])
        for h in heads:
            s_next = logits(h + 1) if h + 1 in heads else None
            m_old = mrow[h, :, qs]
            m_new = jnp.maximum(m_old, jnp.max(s, axis=0, keepdims=True))
            p = jnp.exp2((s - m_new) * scale)
            a = jnp.exp2((m_old - m_new) * scale)
            l_new = lrow[h, :, qs] * a + jnp.sum(p, axis=0, keepdims=True)
            o_new = acc[h, :, qs] * a + dot_t(vb[:, h * HEAD:(h + 1) * HEAD], p.astype(BF16))
            if out is None:
                lrow[h, :, qs] = l_new
                mrow[h, :, qs] = m_new
                acc[h, :, qs] = o_new
            else:
                out[h * HEAD:(h + 1) * HEAD, :] = (o_new * (1.0 / l_new)).astype(BF16)
            s = s_next

    wq_copy.wait()
    project_q(0)
    wk_copy.wait()
    wv_copy.wait()
    wo_copy.start()
    project(0)
    pair_copy.wait_recv()
    project_q(1)
    project(1)
    arrive(0)
    attend(0)
    twins(0)
    project(2)
    arrive(1)
    attend(1)
    twins(1)
    project(3)
    attend(2)
    arrive(2)
    twins(2)
    project(4)
    attend(3)
    arrive(3)
    attend(4, range(0, 3))
    twins(3)
    project(5)
    attend(4, range(3, 6))
    attend(5, range(0, 3))
    arrive(4)
    attend(5, range(3, 6))
    twins(4)
    project(6)
    arrive(5)
    attend(6)
    arrive(6)
    twins(5)
    project_first(7)
    twins(6)
    project_second(7)
    attend(7, qs=slice(tok, 2 * tok), out=osend)
    wo_copy.wait()
    ocopy = remote(osend, oother, osend_sem, orecv_sem, partner)
    ocopy.start()
    attend(7, qs=slice(0, tok), out=oown)
    own_rows_w = pl.ds(pl.multiple_of(core * half, HEAD), half)
    other_rows_w = pl.ds(pl.multiple_of((1 - core) * half, HEAD), half)
    facc[...] = dot_t(oown[...], wo[own_rows_w, :])
    ocopy.wait_recv()
    y_ref[...] = (facc[...] + dot_t(oother[...], wo[other_rows_w, :])).astype(BF16)

    sent = xbuf.at[0:7]
    remote(sent, sent, send_sem, pair_sem, partner).wait_send()
    ocopy.wait_send()


def solution(mesh):
    def block(x, w_qkv, w_o):
        tok, width = x.shape[1], x.shape[2]
        half = width // 2
        nh = half // HEAD
        any_spec = pl.BlockSpec(memory_space=pl.ANY)
        dma = pltpu.SemaphoreType.DMA
        y = pl.pallas_call(
            kernel,
            out_shape=jax.ShapeDtypeStruct((tok, width), BF16),
            in_specs=[any_spec] * 3,
            out_specs=pl.BlockSpec(memory_space=pltpu.VMEM),
            scratch_shapes=[
                pltpu.VMEM((8, tok, width), BF16),
                pltpu.VMEM((width, half), BF16),
                pltpu.VMEM((width, half), BF16),
                pltpu.VMEM((width, half), BF16),
                pltpu.VMEM((width, width), BF16),
                pltpu.VMEM((nh, HEAD, 2 * tok), BF16),
                pltpu.VMEM((tok, half), BF16),
                pltpu.VMEM((tok, half), BF16),
                pltpu.VMEM((tok, half), BF16),
                pltpu.VMEM((tok, half), BF16),
                pltpu.VMEM((nh, HEAD, 2 * tok), F32),
                pltpu.VMEM((nh, 1, 2 * tok), F32),
                pltpu.VMEM((nh, 1, 2 * tok), F32),
                pltpu.VMEM((half, tok), BF16),
                pltpu.VMEM((half, tok), BF16),
                pltpu.VMEM((half, tok), BF16),
                pltpu.VMEM((tok, width), F32),
                dma((4,)), dma((2,)), dma(()), dma(()), dma(()), dma((7,)), dma((7,)), dma(()),
            ],
            compiler_params=pltpu.CompilerParams(
                collective_id=0, has_side_effects=True, vmem_limit_bytes=53 * 1024 * 1024),
            name="gather_attend",
        )(x[0], w_qkv, w_o.reshape(width, width))
        return y[None]

    return jax.shard_map(
        block, mesh=mesh,
        in_specs=(P("dp", ("cx", "cy"), None), P(None, None), P(None, None, None)),
        out_specs=P("dp", ("cx", "cy"), None), check_vma=False)
```

time: 164 us -> 39 us (0.24)
  blocking collectives: 49.9 us -> 0 us
  waiting for transfers between devices: 43 us -> 0 us
  Pallas kernels: 0 us -> 38 us
  matrix products: 37.1 us -> 0 us
  between operations: 13.5 us -> 0.01 us
  other arithmetic: 11 us -> 0 us
  local copies, waits for them, and re-layouts: 9.41 us -> 0.88 us
    all_to_all x2 -> x0, blocking collectives: 49.9 us -> none  [the longest x1 32.9 us: attend_local(): lax.all_to_all(qkv_rows.reshape(tok_rows, 3, num_heads, head_dim), 'cy',...]
    all_gather x1 -> x0, waiting for transfers between devices: 43 us -> none  [attend_local(): kv_all = lax.all_gather(qkv_rows[:, 1:], 'cx', axis=0, tiled=True)]
    pallas_call x0 -> x1, Pallas kernels: none -> 38 us  [block(): pl.pallas_call(kernel, out_shape=jax.ShapeDtypeStruct((tok, width), BF16)...]
    dot_general x4 -> x0, matrix products: 37.1 us -> none  [the longest x1 11.5 us: attend_local(): jnp.einsum('qhd,khd->hqk', qkv_rows[:, 0], kv_all[:, 0], preferred_elemen...]
    reduce_sum x1 -> x0, other arithmetic: 11 us -> none  [attend_local(): row_sum = jnp.sum(weights, axis=-1, keepdims=True)]
    convert_element_type x2 -> x0, local copies, waits for them, and re-layouts: 3.56 us -> none  [the longest x1 2.83 us: attend_local(): jnp.dot(x_blk[0], w_qkv, preferred_element_type=jnp.float32)]
    all_to_all x2 -> x0, local copies, waits for them, and re-layouts: 3.2 us -> none  [the longest x1 3.05 us: attend_local(): lax.all_to_all(qkv_rows.reshape(tok_rows, 3, num_heads, head_dim), 'cy',...]
  transfers between devices with their start and end apart: 1 -> 0, of which waited for: 1 -> 0; matrix products, arithmetic and copies ran while one was open for 0% -> 0% of each run, Pallas kernels for 0% -> 0%
where the time goes in v5:
time: 39 us; the launch traced here: 38.9 us
  Pallas kernels  38 us (97%)
  local copies, waits for them, and re-layouts  0.88 us (2%)
    pallas_call x1, Pallas kernels, block(): pl.pallas_call(kernel, out_shape=jax.ShapeDtypeStruct((tok, width), BF16)...  38 us
    unnamed x1, local copies, waits for them, and re-layouts  0.88 us

profile of v5, /device:TPU:0, one launch (start us, length us, event | category | flops | bytes accessed | tf_op | source)
XLA Modules:
  0.0 38.9 jit_solution(14335631814547832092)
XLA Ops:
  0.0 38.0 %gather_attend.1 = bf16[256,1536]{1,0:T(8,128)(2,1)S(1)} custom-call(bf16[256,1536]{1,0:T(8,128)(2,1)} %bitcast.5, bf16[1536,4608]{1,0:T(8,128)(2,1)} %wqkv_hbm.1, bf16[1536,1536]{1,0:T(8,128)(2,1)} %bitcast.4), custom_call_target="tpu_custom_call" | custom-call | tf_op jit(solution)/shard_map/gather_attend/pallas_call | solution.py:221
  38.0 0.9 %copy.5 = bf16[1,256,1536]{2,1,0:T(8,128)(2,1)} copy(bf16[1,256,1536]{2,1,0:T(8,128)(2,1)S(1)} %bitcast.3) | data formatting | bytes 1572864

commit v6 on v5

--- a/solution.py
+++ b/solution.py
@@ -19,6 +19,7 @@
     half = width // 2
     nh = half // HEAD
     quarter = tok // 4
+    cut = 9 * HEAD
     scale = math.log2(math.e) / math.sqrt(HEAD)
 
     dp, cx, cy = lax.axis_index("dp"), lax.axis_index("cx"), lax.axis_index("cy")
@@ -53,7 +54,7 @@
     xload_wait(0)
     pl.semaphore_wait(barrier, 3)
 
-    pieces = [(c, slice(0, width)) for c in range(2, 7)] + [(7, slice(0, half)), (7, slice(half, width))]
+    pieces = [(c, slice(0, width)) for c in range(2, 7)] + [(7, slice(0, cut)), (7, slice(cut, width))]
 
     def part(c, q, cols):
         return xbuf.at[c, q * quarter:(q + 1) * quarter, cols]
@@ -92,15 +93,16 @@
         both_parts(i, link_sem).wait_recv()
         twin_copy(i, 0).start()
         twin_copy(i, 2).start()
-        send(i + depth)
+        if i == 1:
+            send(i + 2)
+        send(i + depth - (i < 1))
 
     def twins(i):
         both_parts(i, twin_sem).wait_recv()
 
     send(0)
     xload_wait(1)
-    for i in range(1, depth):
-        send(i)
+    send(1)
     pair_copy.start()
     wk_copy.start()
     wv_copy.start()
@@ -114,9 +116,9 @@
     kbufs, vbufs = (kbuf0, kbuf1), (vbuf0, vbuf1)
 
     def project_q(c):
-        q = dot(xbuf[c], wq[...])
+        q = dot(xbuf[c], wq[...]).astype(BF16)
         for h in range(nh):
-            qt[h, :, c * tok:(c + 1) * tok] = q[:, h * HEAD:(h + 1) * HEAD].T.astype(BF16)
+            qt[h, :, c * tok:(c + 1) * tok] = q[:, h * HEAD:(h + 1) * HEAD].T
 
     def project(c):
         xs = xbuf[c]
@@ -124,36 +126,38 @@
         vbufs[c % 2][...] = dot(xs, wv[...]).astype(BF16)
 
     def project_first(c):
-        xs = xbuf[c, :, 0:half]
-        facc[:, 0:half] = dot(xs, wk[0:half, :])
-        facc[:, half:] = dot(xs, wv[0:half, :])
+        xs = xbuf[c, :, 0:cut]
+        facc[:, 0:half] = dot(xs, wk[0:cut, :])
+        facc[:, half:] = dot(xs, wv[0:cut, :])
 
     def project_second(c):
-        xs = xbuf[c, :, half:]
-        kbufs[c % 2][...] = (facc[:, 0:half] + dot(xs, wk[half:, :])).astype(BF16)
-        vbufs[c % 2][...] = (facc[:, half:] + dot(xs, wv[half:, :])).astype(BF16)
-
-    def attend(c, heads=range(nh), qs=slice(0, 2 * tok), out=None):
+        xs = xbuf[c, :, cut:]
+        kbufs[c % 2][...] = (facc[:, 0:half] + dot(xs, wk[cut:, :])).astype(BF16)
+        vbufs[c % 2][...] = (facc[:, half:] + dot(xs, wv[cut:, :])).astype(BF16)
+
+    def attend(c, heads=range(nh), last=False):
         kb, vb = kbufs[c % 2], vbufs[c % 2]
 
         def logits(h):
-            return dot(kb[:, h * HEAD:(h + 1) * HEAD], qt[h, :, qs])
+            return dot(kb[:, h * HEAD:(h + 1) * HEAD], qt[h])
 
         s = logits(heads[0])
         for h in heads:
             s_next = logits(h + 1) if h + 1 in heads else None
-            m_old = mrow[h, :, qs]
+            m_old = mrow[h]
             m_new = jnp.maximum(m_old, jnp.max(s, axis=0, keepdims=True))
             p = jnp.exp2((s - m_new) * scale)
             a = jnp.exp2((m_old - m_new) * scale)
-            l_new = lrow[h, :, qs] * a + jnp.sum(p, axis=0, keepdims=True)
-            o_new = acc[h, :, qs] * a + dot_t(vb[:, h * HEAD:(h + 1) * HEAD], p.astype(BF16))
-            if out is None:
-                lrow[h, :, qs] = l_new
-                mrow[h, :, qs] = m_new
-                acc[h, :, qs] = o_new
+            l_new = lrow[h] * a + jnp.sum(p, axis=0, keepdims=True)
+            o_new = acc[h] * a + dot_t(vb[:, h * HEAD:(h + 1) * HEAD], p.astype(BF16))
+            if not last:
+                lrow[h] = l_new
+                mrow[h] = m_new
+                acc[h] = o_new
             else:
-                out[h * HEAD:(h + 1) * HEAD, :] = (o_new * (1.0 / l_new)).astype(BF16)
+                o = (o_new * (1.0 / l_new)).astype(BF16)
+                oown[h * HEAD:(h + 1) * HEAD, :] = o[:, 0:tok]
+                osend[h * HEAD:(h + 1) * HEAD, :] = o[:, tok:]
             s = s_next
 
     wq_copy.wait()
@@ -175,14 +179,14 @@
     project(3)
     attend(2)
     arrive(2)
+    attend(3)
     twins(2)
     project(4)
-    attend(3)
+    attend(4, range(0, 3))
     arrive(3)
-    attend(4, range(0, 3))
+    attend(4, range(3, 6))
     twins(3)
     project(5)
-    attend(4, range(3, 6))
     attend(5, range(0, 3))
     arrive(4)
     attend(5, range(3, 6))
@@ -195,20 +199,29 @@
     project_first(7)
     twins(6)
     project_second(7)
-    attend(7, qs=slice(tok, 2 * tok), out=osend)
+
+    def ocopy(i):
+        rows = slice(i * half // 2, (i + 1) * half // 2)
+        return remote(osend.at[rows, :], oother.at[rows, :], osend_sem, orecv_sem.at[i], partner)
+
+    attend(7, range(0, 3), last=True)
+    ocopy(0).start()
+    attend(7, range(3, 6), last=True)
+    ocopy(1).start()
     wo_copy.wait()
-    ocopy = remote(osend, oother, osend_sem, orecv_sem, partner)
-    ocopy.start()
-    attend(7, qs=slice(0, tok), out=oown)
-    own_rows_w = pl.ds(pl.multiple_of(core * half, HEAD), half)
-    other_rows_w = pl.ds(pl.multiple_of((1 - core) * half, HEAD), half)
-    facc[...] = dot_t(oown[...], wo[own_rows_w, :])
-    ocopy.wait_recv()
-    y_ref[...] = (facc[...] + dot_t(oother[...], wo[other_rows_w, :])).astype(BF16)
+    hh = half // 2
+
+    def wo_rows(start, n):
+        return wo[pl.ds(pl.multiple_of(start, HEAD), n), :]
+
+    ocopy(0).wait_recv()
+    facc[...] = dot_t(oown[...], wo_rows(core * half, half)) + dot_t(oother[0:hh, :], wo_rows((1 - core) * half, hh))
+    ocopy(1).wait_recv()
+    y_ref[...] = (facc[...] + dot_t(oother[hh:, :], wo_rows((1 - core) * half + hh, hh))).astype(BF16)
 
     sent = xbuf.at[0:7]
     remote(sent, sent, send_sem, pair_sem, partner).wait_send()
-    ocopy.wait_send()
+    remote(osend, osend, osend_sem, pair_sem, partner).wait_send()
 
 
 def solution(mesh):
@@ -241,7 +254,7 @@
                 pltpu.VMEM((half, tok), BF16),
                 pltpu.VMEM((half, tok), BF16),
                 pltpu.VMEM((tok, width), F32),
-                dma((4,)), dma((2,)), dma(()), dma(()), dma(()), dma((7,)), dma((7,)), dma(()),
+                dma((4,)), dma((2,)), dma(()), dma(()), dma(()), dma((7,)), dma((7,)), dma((2,)),
             ],
             compiler_params=pltpu.CompilerParams(
                 collective_id=0, has_side_effects=True, vmem_limit_bytes=53 * 1024 * 1024),

time: 39 us -> 38.4 us (0.985)
  Pallas kernels: 38 us -> 37.4 us
    pallas_call x1, Pallas kernels: 38 us -> 37.4 us  [block(): pl.pallas_call(kernel, out_shape=jax.ShapeDtypeStruct((tok, width), BF16)...]
where the time goes in v6:
time: 38.4 us; the launch traced here: 38.3 us
  Pallas kernels  37.4 us (97%)
  local copies, waits for them, and re-layouts  0.88 us (2%)
    pallas_call x1, Pallas kernels, block(): pl.pallas_call(kernel, out_shape=jax.ShapeDtypeStruct((tok, width), BF16)...  37.4 us
    unnamed x1, local copies, waits for them, and re-layouts  0.88 us

profile of v6, /device:TPU:0, one launch (start us, length us, event | category | flops | bytes accessed | tf_op | source)
XLA Modules:
  0.0 38.3 jit_solution(11640505507855599161)
XLA Ops:
  0.0 37.4 %gather_attend.1 = bf16[256,1536]{1,0:T(8,128)(2,1)S(1)} custom-call(bf16[256,1536]{1,0:T(8,128)(2,1)} %bitcast.5, bf16[1536,4608]{1,0:T(8,128)(2,1)} %wqkv_hbm.1, bf16[1536,1536]{1,0:T(8,128)(2,1)} %bitcast.4), custom_call_target="tpu_custom_call" | custom-call | tf_op jit(solution)/shard_map/gather_attend/pallas_call | solution.py:234
  37.4 0.9 %copy.5 = bf16[1,256,1536]{2,1,0:T(8,128)(2,1)} copy(bf16[1,256,1536]{2,1,0:T(8,128)(2,1)S(1)} %bitcast.3) | data formatting | bytes 1572864

commit v7 on v6

--- a/solution.py
+++ b/solution.py
@@ -100,9 +100,16 @@
     def twins(i):
         both_parts(i, twin_sem).wait_recv()
 
-    send(0)
+    @pl.when(core == 0)
+    def _():
+        send(0)
+
     xload_wait(1)
-    send(1)
+
+    @pl.when(core == 0)
+    def _():
+        send(1)
+
     pair_copy.start()
     wk_copy.start()
     wv_copy.start()
@@ -161,6 +168,12 @@
             s = s_next
 
     wq_copy.wait()
+
+    @pl.when(core == 1)
+    def _():
+        send(0)
+        send(1)
+
     project_q(0)
     wk_copy.wait()
     wv_copy.wait()

time: 38.4 us -> 38.7 us (level)
  no operation moved by 1% of the time
where the time goes in v7:
time: 38.7 us; the launch traced here: 38.6 us
  Pallas kernels  37.7 us (97%)
  local copies, waits for them, and re-layouts  0.88 us (2%)
    pallas_call x1, Pallas kernels, block(): pl.pallas_call(kernel, out_shape=jax.ShapeDtypeStruct((tok, width), BF16)...  37.7 us
    unnamed x1, local copies, waits for them, and re-layouts  0.88 us

profile of v7, /device:TPU:0, one launch (start us, length us, event | category | flops | bytes accessed | tf_op | source)
XLA Modules:
  0.0 38.6 jit_solution(3175482086724008373)
XLA Ops:
  0.0 37.7 %gather_attend.1 = bf16[256,1536]{1,0:T(8,128)(2,1)S(1)} custom-call(bf16[256,1536]{1,0:T(8,128)(2,1)} %bitcast.5, bf16[1536,4608]{1,0:T(8,128)(2,1)} %wqkv_hbm.1, bf16[1536,1536]{1,0:T(8,128)(2,1)} %bitcast.4), custom_call_target="tpu_custom_call" | custom-call | tf_op jit(solution)/shard_map/gather_attend/pallas_call | solution.py:247
  37.7 0.9 %copy.5 = bf16[1,256,1536]{2,1,0:T(8,128)(2,1)} copy(bf16[1,256,1536]{2,1,0:T(8,128)(2,1)S(1)} %bitcast.3) | data formatting | bytes 1572864

commit v8 on v7

--- a/solution.py
+++ b/solution.py
@@ -110,7 +110,10 @@
     def _():
         send(1)
 
-    pair_copy.start()
+    @pl.when(core == 1)
+    def _():
+        pair_copy.start()
+
     wk_copy.start()
     wv_copy.start()
 
@@ -168,6 +171,10 @@
             s = s_next
 
     wq_copy.wait()
+
+    @pl.when(core == 0)
+    def _():
+        pair_copy.start()
 
     @pl.when(core == 1)
     def _():

time: 38.7 us -> 38.7 us (level)
  no operation moved by 1% of the time
where the time goes in v8:
time: 38.7 us; the launch traced here: 38.6 us
  Pallas kernels  37.7 us (97%)
  local copies, waits for them, and re-layouts  0.88 us (2%)
    pallas_call x1, Pallas kernels, block(): pl.pallas_call(kernel, out_shape=jax.ShapeDtypeStruct((tok, width), BF16)...  37.7 us
    unnamed x1, local copies, waits for them, and re-layouts  0.88 us

profile of v8, /device:TPU:0, one launch (start us, length us, event | category | flops | bytes accessed | tf_op | source)
XLA Modules:
  0.0 38.6 jit_solution(11254833688286355139)
XLA Ops:
  0.0 37.7 %gather_attend.1 = bf16[256,1536]{1,0:T(8,128)(2,1)S(1)} custom-call(bf16[256,1536]{1,0:T(8,128)(2,1)} %bitcast.5, bf16[1536,4608]{1,0:T(8,128)(2,1)} %wqkv_hbm.1, bf16[1536,1536]{1,0:T(8,128)(2,1)} %bitcast.4), custom_call_target="tpu_custom_call" | custom-call | tf_op jit(solution)/shard_map/gather_attend/pallas_call | solution.py:254
  37.7 0.9 %copy.5 = bf16[1,256,1536]{2,1,0:T(8,128)(2,1)} copy(bf16[1,256,1536]{2,1,0:T(8,128)(2,1)S(1)} %bitcast.3) | data formatting | bytes 1572864

commit v9 on v6

--- a/solution.py
+++ b/solution.py
@@ -69,12 +69,12 @@
         if c < 6:
             src = own_rows((c if q == 0 else c - 2) % 4)
         else:
-            src = part(c - 4, 2 - q, cols)
+            src = part(c - 4, 1 - q, cols)
         return remote(src, part(c, q, cols), send_sem, link_sem.at[i], dev)
 
     def twin_copy(i, q):
         c, cols = pieces[i]
-        return remote(part(c, q, cols), part(c, q + 1, cols), send_sem, twin_sem.at[i], partner)
+        return remote(part(c, q, cols), part(c, q + 2, cols), send_sem, twin_sem.at[i], partner)
 
     pair_copy = remote(xbuf.at[0], xbuf.at[1], send_sem, pair_sem, partner)
     depth = 3
@@ -82,7 +82,7 @@
     def send(i):
         if i < len(pieces):
             link_copy(i, 0).start()
-            link_copy(i, 2).start()
+            link_copy(i, 1).start()
 
     def both_parts(i, sems):
         c, cols = pieces[i]
@@ -92,7 +92,7 @@
     def arrive(i):
         both_parts(i, link_sem).wait_recv()
         twin_copy(i, 0).start()
-        twin_copy(i, 2).start()
+        twin_copy(i, 1).start()
         if i == 1:
             send(i + 2)
         send(i + depth - (i < 1))
@@ -120,10 +120,10 @@
         for h in range(nh):
             qt[h, :, c * tok:(c + 1) * tok] = q[:, h * HEAD:(h + 1) * HEAD].T
 
-    def project(c):
-        xs = xbuf[c]
-        kbufs[c % 2][...] = dot(xs, wk[...]).astype(BF16)
-        vbufs[c % 2][...] = dot(xs, wv[...]).astype(BF16)
+    def project(c, lo=0, hi=tok):
+        xs = xbuf[c, lo:hi, :]
+        kbufs[c % 2][lo:hi, :] = dot(xs, wk[...]).astype(BF16)
+        vbufs[c % 2][lo:hi, :] = dot(xs, wv[...]).astype(BF16)
 
     def project_first(c):
         xs = xbuf[c, :, 0:cut]
@@ -189,9 +189,10 @@
     project(5)
     attend(5, range(0, 3))
     arrive(4)
+    project(6, 0, tok // 2)
     attend(5, range(3, 6))
     twins(4)
-    project(6)
+    project(6, tok // 2, tok)
     arrive(5)
     attend(6)
     arrive(6)
@@ -200,24 +201,28 @@
     twins(6)
     project_second(7)
 
+    first = 4
+
     def ocopy(i):
-        rows = slice(i * half // 2, (i + 1) * half // 2)
+        rows = slice(0, first * HEAD) if i == 0 else slice(first * HEAD, half)
         return remote(osend.at[rows, :], oother.at[rows, :], osend_sem, orecv_sem.at[i], partner)
 
-    attend(7, range(0, 3), last=True)
+    attend(7, range(0, first), last=True)
     ocopy(0).start()
-    attend(7, range(3, 6), last=True)
+    attend(7, range(first, nh), last=True)
     ocopy(1).start()
     wo_copy.wait()
-    hh = half // 2
 
     def wo_rows(start, n):
         return wo[pl.ds(pl.multiple_of(start, HEAD), n), :]
 
+    cutrow = first * HEAD
+    other = (1 - core) * half
+    facc[...] = dot_t(oown[...], wo_rows(core * half, half))
     ocopy(0).wait_recv()
-    facc[...] = dot_t(oown[...], wo_rows(core * half, half)) + dot_t(oother[0:hh, :], wo_rows((1 - core) * half, hh))
+    facc[...] += dot_t(oother[0:cutrow, :], wo_rows(other, cutrow))
     ocopy(1).wait_recv()
-    y_ref[...] = (facc[...] + dot_t(oother[hh:, :], wo_rows((1 - core) * half + hh, hh))).astype(BF16)
+    y_ref[...] = (facc[...] + dot_t(oother[cutrow:, :], wo_rows(other + cutrow, half - cutrow))).astype(BF16)
 
     sent = xbuf.at[0:7]
     remote(sent, sent, send_sem, pair_sem, partner).wait_send()

time: 38.4 us -> 37.6 us (0.979)
  Pallas kernels: 37.4 us -> 36.6 us
    pallas_call x1, Pallas kernels: 37.4 us -> 36.6 us  [block(): pl.pallas_call(kernel, out_shape=jax.ShapeDtypeStruct((tok, width), BF16)...]
where the time goes in v9:
time: 37.6 us; the launch traced here: 37.5 us
  Pallas kernels  36.6 us (97%)
  local copies, waits for them, and re-layouts  0.88 us (2%)
    pallas_call x1, Pallas kernels, block(): pl.pallas_call(kernel, out_shape=jax.ShapeDtypeStruct((tok, width), BF16)...  36.6 us
    unnamed x1, local copies, waits for them, and re-layouts  0.88 us

profile of v9, /device:TPU:0, one launch (start us, length us, event | category | flops | bytes accessed | tf_op | source)
XLA Modules:
  0.0 37.5 jit_solution(3297461204951995293)
XLA Ops:
  0.0 36.6 %gather_attend.1 = bf16[256,1536]{1,0:T(8,128)(2,1)S(1)} custom-call(bf16[256,1536]{1,0:T(8,128)(2,1)} %bitcast.5, bf16[1536,4608]{1,0:T(8,128)(2,1)} %wqkv_hbm.1, bf16[1536,1536]{1,0:T(8,128)(2,1)} %bitcast.4), custom_call_target="tpu_custom_call" | custom-call | tf_op jit(solution)/shard_map/gather_attend/pallas_call | solution.py:239
  36.6 0.9 %copy.5 = bf16[1,256,1536]{2,1,0:T(8,128)(2,1)} copy(bf16[1,256,1536]{2,1,0:T(8,128)(2,1)S(1)} %bitcast.3) | data formatting | bytes 1572864

commit v10 on v9

--- a/solution.py
+++ b/solution.py
@@ -72,9 +72,13 @@
             src = part(c - 4, 1 - q, cols)
         return remote(src, part(c, q, cols), send_sem, link_sem.at[i], dev)
 
-    def twin_copy(i, q):
+    def twin_copies(i):
         c, cols = pieces[i]
-        return remote(part(c, q, cols), part(c, q + 2, cols), send_sem, twin_sem.at[i], partner)
+        n = 2 * quarter // 8
+        for r in range(8):
+            src = xbuf.at[c, r * n:(r + 1) * n, cols]
+            dst = xbuf.at[c, 2 * quarter + r * n:2 * quarter + (r + 1) * n, cols]
+            remote(src, dst, send_sem, twin_sem.at[i], partner).start()
 
     pair_copy = remote(xbuf.at[0], xbuf.at[1], send_sem, pair_sem, partner)
     depth = 3
@@ -91,8 +95,7 @@
 
     def arrive(i):
         both_parts(i, link_sem).wait_recv()
-        twin_copy(i, 0).start()
-        twin_copy(i, 1).start()
+        twin_copies(i)
         if i == 1:
             send(i + 2)
         send(i + depth - (i < 1))

time: 37.6 us -> 37.6 us (level)
  no operation moved by 1% of the time
where the time goes in v10:
time: 37.6 us; the launch traced here: 37.5 us
  Pallas kernels  36.6 us (97%)
  local copies, waits for them, and re-layouts  0.88 us (2%)
    pallas_call x1, Pallas kernels, block(): pl.pallas_call(kernel, out_shape=jax.ShapeDtypeStruct((tok, width), BF16)...  36.6 us
    unnamed x1, local copies, waits for them, and re-layouts  0.88 us

profile of v10, /device:TPU:0, one launch (start us, length us, event | category | flops | bytes accessed | tf_op | source)
XLA Modules:
  0.0 37.5 jit_solution(7332741336964852260)
XLA Ops:
  0.0 36.6 %gather_attend.1 = bf16[256,1536]{1,0:T(8,128)(2,1)S(1)} custom-call(bf16[256,1536]{1,0:T(8,128)(2,1)} %bitcast.5, bf16[1536,4608]{1,0:T(8,128)(2,1)} %wqkv_hbm.1, bf16[1536,1536]{1,0:T(8,128)(2,1)} %bitcast.4), custom_call_target="tpu_custom_call" | custom-call | tf_op jit(solution)/shard_map/gather_attend/pallas_call | solution.py:242
  36.6 0.9 %copy.5 = bf16[1,256,1536]{2,1,0:T(8,128)(2,1)} copy(bf16[1,256,1536]{2,1,0:T(8,128)(2,1)S(1)} %bitcast.3) | data formatting | bytes 1572864
